TPU v7x, 32 devices: a whole 2x2x4 slice. The times are simulated.
32 devices in a mesh: fsdp: 8 (over z, core), tp: 4 (over y, x).
Axes of the slice: x: 2, y: 2, z: 4, core: 2. Of those that a mesh axis runs over, the one named last changes fastest.
Arguments:
- hidden_in: bfloat16 [512, 4096], P('fsdp'), may hold values from -3 to 3
- queries: bfloat16 [2, 512, 8192], P(None, ('fsdp', 'tp')), may hold values from -170 to 170
- key_cache: bfloat16 [512, 256, 512], P(('fsdp', 'tp')), may hold values from -6 to 6
- value_cache: bfloat16 [512, 256, 512], P(('fsdp', 'tp')), may hold values from -6 to 6
- new_keys: bfloat16 [2, 512, 512], P(None, ('fsdp', 'tp')), may hold values from -6 to 6
- new_values: bfloat16 [2, 512, 512], P(None, ('fsdp', 'tp')), may hold values from -6 to 6
- lengths: int32 [512], P(('fsdp', 'tp')), may hold values from 2 to 256
- routes: int32 [2, 512, 8], P(None, 'fsdp'), may hold values from 0 to 127, all different within a row; in each aligned block of 64 rows (0 to 63, 64 to 127, ..., all dimensions but the last counted through in order) at most 8 rows name the same one
- route_weights: float32 [2, 512, 8], P(None, 'fsdp'), may hold values from 0.05 to 1
- norm_gain: float32 [4096], replicated, may hold values from 0.1 to 1.9
- gate_master: float32 [8, 1536, 4096], P(None, ('fsdp', 'tp')), may hold values from -0.09375 to 0.09375
- up_master: float32 [8, 1536, 4096], P(None, ('fsdp', 'tp')), may hold values from -0.09375 to 0.09375
- down_master: float32 [8, 1536, 4096], P(None, ('fsdp', 'tp')), may hold values from -0.3125 to 0.3125
- out_proj: bfloat16 [8192, 4096], P('tp'), may hold values from -0.0625 to 0.0625
Outputs:
- hidden_out: bfloat16 [512, 4096], P('fsdp', 'tp')
- scale_log2: float32 [3, 8, 12, 32], replicated
Inputs may be any that keep to these rules, and one draw needn't show every extreme that they name: `routes`: within one step and one index of fsdp (aligned blocks of 64 rows), no expert is named by more than 8 rows.
All inputs are finite; a program needn't handle non-finite values.
Results may differ from a plain program's by a relative error of at most 0.0095.
Values may be sent and summed in bfloat16 or wider, within the bound.
No kernel may reach another device: no remote copies, remote signals or barrier semaphores. Data moves between devices by JAX's collectives and lax.ppermute only.
A program may use at most 384 MiB of HBM per device.

v0:
```python
import jax
import jax.numpy as jnp
from jax import lax
from jax.sharding import PartitionSpec as P

D = 4096
FF = 1536
QH = 64
KVH = 4
HD = 128
BLOCK = 128
WIN = 8
CAP = 8
neg_fill = -1e30
epsilon = 1e-06
fp_limit = 448.0
grid_floor = 2.0 ** (-10)
least_exponent = -6.0


def grid_round(values):
    magnitude = jnp.abs(values)
    exponent = jnp.maximum(jnp.floor(jnp.log2(jnp.maximum(magnitude, grid_floor))), least_exponent)
    spacing = jnp.exp2(exponent - 3.0)
    return jnp.sign(values) * jnp.floor(magnitude / spacing + 0.5) * spacing


def row_scales(scales, owner_map):
    return jnp.einsum(
        "sb,xwbc->xwsc", owner_map.astype(jnp.float32), scales, precision=lax.Precision.HIGHEST
    )


def owner_blocks(owner_rows):
    return (owner_rows // BLOCK)[:, None] == jnp.arange(FF // BLOCK, dtype=jnp.int32)[None, :]


def dequantize(shard_piece, shard_rows, tp_count, tp_pos, scales):
    count = shard_piece.shape[2]
    gathered_index = jnp.arange(count, dtype=jnp.int32)
    owner_rows = (
        gathered_index // shard_rows * tp_count + tp_pos
    ) * shard_rows + gathered_index % shard_rows
    factors = row_scales(scales, owner_blocks(owner_rows))
    tiles = shard_piece.astype(jnp.float32).reshape(3, WIN, count, D // BLOCK, BLOCK)
    return (tiles * factors[..., None]).astype(jnp.bfloat16).reshape(3, WIN, count, D)


def attention_rows(queries_now, cache_keys, cache_values, fresh_keys, fresh_values, lengths):
    row_count = queries_now.shape[0]
    positions = cache_keys.shape[1]
    group = QH // KVH
    score_scale = HD ** (-0.5)
    fresh_count = fresh_keys.shape[0]
    query_heads = queries_now.reshape(row_count, KVH, group, HD)
    key_heads = cache_keys.reshape(row_count, positions, KVH, HD)
    value_heads = cache_values.reshape(row_count, positions, KVH, HD)
    fresh_key_heads = fresh_keys.reshape(fresh_count, row_count, KVH, HD)
    fresh_value_heads = fresh_values.reshape(fresh_count, row_count, KVH, HD)
    cached_scores = (
        jnp.einsum("rkgd,rpkd->rkgp", query_heads, key_heads, preferred_element_type=jnp.float32)
        * score_scale
    )
    fresh_scores = (
        jnp.einsum(
            "rkgd,srkd->rkgs", query_heads, fresh_key_heads, preferred_element_type=jnp.float32
        )
        * score_scale
    )
    alive_mask = (jnp.arange(positions, dtype=jnp.int32)[None, :] < lengths[:, None])[
        :, None, None, :
    ]
    peak_score = jnp.maximum(
        jnp.max(jnp.where(alive_mask, cached_scores, neg_fill), axis=-1),
        jnp.max(fresh_scores, axis=-1),
    )
    cached_weights = jnp.where(alive_mask, jnp.exp(cached_scores - peak_score[..., None]), 0.0)
    fresh_weights = jnp.exp(fresh_scores - peak_score[..., None])
    weight_sum = jnp.sum(cached_weights, axis=-1) + jnp.sum(fresh_weights, axis=-1)
    cached_probs = (cached_weights / weight_sum[..., None]).astype(jnp.bfloat16)
    fresh_probs = (fresh_weights / weight_sum[..., None]).astype(jnp.bfloat16)
    output = jnp.einsum(
        "rkgp,rpkd->rkgd", cached_probs, value_heads, preferred_element_type=jnp.float32
    )
    output = output + jnp.einsum(
        "rkgs,srkd->rkgd", fresh_probs, fresh_value_heads, preferred_element_type=jnp.float32
    )
    return output.astype(jnp.bfloat16).reshape(row_count, QH * HD)


def routing_tables(routes, route_weights, capacity):
    weight_sum = jnp.sum(route_weights, axis=1)
    experts = jnp.arange(WIN, dtype=jnp.int32)
    matches = routes[None, :, :] == experts[:, None, None]
    chosen = jnp.any(matches, axis=2)
    gate_share = (
        jnp.sum(jnp.where(matches, route_weights[None, :, :], 0.0), axis=2) / weight_sum[None, :]
    )
    slot_index = jnp.cumsum(chosen.astype(jnp.int32), axis=1) - 1
    places = jnp.arange(capacity, dtype=jnp.int32)
    picked = (slot_index[:, None, :] == places[None, :, None]) & chosen[:, None, :]
    return (picked.astype(jnp.bfloat16), picked.astype(jnp.float32) * gate_share[:, None, :])


def expert_rows(selected, gate_rows, up_rows, down_rows):
    gate_act = jnp.einsum("ecd,ehd->ech", selected, gate_rows, preferred_element_type=jnp.float32)
    up_act = jnp.einsum("ecd,ehd->ech", selected, up_rows, preferred_element_type=jnp.float32)
    product = (jax.nn.silu(gate_act) * up_act).astype(jnp.bfloat16)
    return jnp.einsum("ech,ehd->ecd", product, down_rows, preferred_element_type=jnp.float32)


def local_experts(selected, weighted, restored):
    outputs = expert_rows(selected, restored[0], restored[1], restored[2])
    return jnp.einsum("ecr,ecd->rd", weighted, outputs, precision=lax.Precision.HIGHEST)


def local(
    hidden_in,
    queries,
    key_cache,
    value_cache,
    new_keys,
    new_values,
    lengths,
    routes,
    route_weights,
    norm_gain,
    gate_master,
    up_master,
    down_master,
    out_proj,
):
    tp_count = lax.axis_size("tp")
    fsdp_pos = lax.axis_index("fsdp")
    tp_pos = lax.axis_index("tp")
    shard_rows = gate_master.shape[1]
    masters = jnp.stack([gate_master, up_master, down_master])
    owned_rows = (fsdp_pos * tp_count + tp_pos) * shard_rows + jnp.arange(
        shard_rows, dtype=jnp.int32
    )
    owner_map = owner_blocks(owned_rows)
    magnitude = jnp.max(jnp.abs(masters).reshape(3, WIN, shard_rows, D // BLOCK, BLOCK), axis=4)
    partial_max = jnp.max(
        jnp.where(owner_map[None, None, :, :, None], magnitude[:, :, :, None, :], 0.0), axis=2
    )
    block_max = lax.pmax(partial_max, ("fsdp", "tp"))
    scales = (block_max + epsilon) / fp_limit
    scale_log2 = jnp.log2(scales)
    local_factors = row_scales(scales, owner_map)
    tiles = masters.reshape(3, WIN, shard_rows, D // BLOCK, BLOCK)
    quantized = (
        grid_round(tiles / local_factors[..., None])
        .astype(jnp.bfloat16)
        .reshape(3, WIN, shard_rows, D)
    )
    gathered = lax.all_gather(quantized, "fsdp", axis=2, tiled=True)
    restored = dequantize(gathered, shard_rows, tp_count, tp_pos, scales)
    share_cols = D // tp_count
    own_start = tp_pos * share_cols
    current = lax.dynamic_slice_in_dim(hidden_in, own_start, share_cols, 1)
    for step_index in range(2):
        heads_local = attention_rows(
            queries[step_index],
            key_cache,
            value_cache,
            new_keys[: step_index + 1],
            new_values[: step_index + 1],
            lengths,
        )
        regrouped = lax.all_to_all(heads_local, "tp", split_axis=1, concat_axis=0, tiled=True)
        projected = jnp.dot(regrouped, out_proj, preferred_element_type=jnp.float32)
        mixed = (
            current.astype(jnp.float32)
            + lax.psum_scatter(projected, "tp", scatter_dimension=1, tiled=True)
        ).astype(jnp.bfloat16)
        values = mixed.astype(jnp.float32)
        squares = lax.psum(jnp.sum(values * values, axis=1), "tp")
        inverse = lax.rsqrt(squares / D + epsilon)
        own_gain = lax.dynamic_slice_in_dim(norm_gain, own_start, share_cols, 0)
        normed_share = (values * inverse[:, None] * own_gain[None, :]).astype(jnp.bfloat16)
        normed = lax.all_gather(normed_share, "tp", axis=1, tiled=True)
        picked, weighted = routing_tables(routes[step_index], route_weights[step_index], CAP)
        selected = jnp.einsum(
            "ecr,rd->ecd", picked, normed, preferred_element_type=jnp.float32
        ).astype(jnp.bfloat16)
        partial_value = local_experts(selected, weighted, restored)
        current = (
            mixed.astype(jnp.float32)
            + lax.psum_scatter(partial_value, "tp", scatter_dimension=1, tiled=True)
        ).astype(jnp.bfloat16)
    return (current, scale_log2)


def solution(mesh):
    in_specs = (
        P("fsdp", None),
        P(None, ("fsdp", "tp"), None),
        P(("fsdp", "tp"), None, None),
        P(("fsdp", "tp"), None, None),
        P(None, ("fsdp", "tp"), None),
        P(None, ("fsdp", "tp"), None),
        P(("fsdp", "tp")),
        P(None, "fsdp", None),
        P(None, "fsdp", None),
        P(),
        P(None, ("fsdp", "tp"), None),
        P(None, ("fsdp", "tp"), None),
        P(None, ("fsdp", "tp"), None),
        P("tp", None),
    )
    out_specs = (P("fsdp", "tp"), P())
    return jax.shard_map(local, mesh=mesh, in_specs=in_specs, out_specs=out_specs, check_vma=False)
```

profile of v0, /device:TPU:0, one launch (start us, length us, event | category | flops | bytes accessed | tf_op | source)
XLA Modules:
  0.0 1244.2 jit_solution(15809943041866484468)
XLA Ops:
  8.0 1.1 slice_bitcast_fusion.1
  9.1 0.8 iota_compare_fusion.5
  9.9 0.7 slice.40
  10.7 0.2 fusion.124
  10.9 3.5 select_reduce_fusion.2
  14.5 0.9 copy-done.5
  15.4 3.5 fusion.37
  19.0 0.9 slice_convert_fusion
  19.9 4.0 fusion.28
  23.9 1.0 all_to_all.28
  24.9 0.9 copy.67
  25.8 5.2 all-to-all-start
  31.0 4.2 copy.90
  35.2 4.1 copy.89
  39.3 1.3 copy.88
  40.6 5.2 fusion
  46.1 1.3 select_reduce_fusion
  47.4 44.0 %pmax.7 = f32[3,8,12,32]{3,2,1,0:T(8,128)S(1)} all-reduce(f32[3,8,12,32]{3,2,1,0:T(8,128)S(1)} %select_reduce_fusion), channel_id=1, replica_groups=mesh['fsdp'=8,'tp'=4] {'fsdp','tp'}, use_global_device_ids=true, to_apply=%region_11.12 | all-reduce | flops 9216 | bytes 73728 | tf_op jit(solution)/shard_map/pmax | solution.py:146
  91.4 0.5 convolution_bitcast_fusion.3
  91.9 0.2 copy.70
  92.1 7.1 div.130
  99.2 20.5 %div.131 = f32[3,8,48,4096]{3,2,1,0:T(8,128)} reshape(f32[3,8,48,32,128]{4,3,2,1,0:T(8,128)} %div.130) | data formatting | bytes 37748736 | tf_op jit(solution)/shard_map/div | solution.py:152
  119.7 9.8 fusion.125
  129.6 22.2 %multiply_convert_fusion.1 = bf16[3,8,48,4096]{3,2,1,0:T(8,128)(2,1)} fusion(f32[3,8,48,4096]{3,2,1,0:T(8,128)} %div.131, f32[1,8,48,4096]{3,2,1,0:T(8,128)} %bitcast.146, f32[1,8,48,4096]{3,2,1,0:T(8,128)} %bitcast.148, f32[1,8,48,4096]{3,2,1,0:T(8,128)} %bitcast.149), kind=kLoop, calls=%fused_computation.4 | loop fusion | flops 80216064 | bytes 47185920 | tf_op jit(solution)/shard_map/convert_element_type | solution.py:153
  151.8 0.3 fusion.123
  152.3 0.4 fusion.38
  152.7 0.3 fusion.74
  153.0 3.0 fusion.25
  156.1 0.9 copy.77
  156.9 3.4 all-to-all-start.1
  160.4 0.7 convolution_bitcast_fusion.2
  161.2 3.9 copy.71
  165.0 0.6 slice_bitcast_fusion.2
  165.7 0.2 reduce_window_sum.17
  165.9 0.7 dynamic_slice.8
  166.6 1.2 slice_reduce_fusion
  167.8 0.6 broadcast_divide_fusion.1
  168.4 13.6 %fusion.127 = f32[64,4096]{1,0:T(8,128)} fusion(bf16[64,2048]{1,0:T(8,128)(2,1)S(1)} %bitcast.154, bf16[2048,4096]{1,0:T(8,128)(2,1)} %param.27), kind=kOutput, calls=%fused_computation.184 | convolution fusion | flops 1073741824 | bytes 18087936 | tf_op jit(solution)/shard_map/dot_general | solution.py:171
  182.2 1.2 fusion.49
  183.4 10.4 psum.14
  193.9 10.0 all_gather.9
  203.9 1.1 convolution_convert_fusion.1
  205.0 579.8 %all-gather.2.cloned.1.call-done = bf16[3,8,384,4096]{3,2,1,0:T(8,128)(2,1)} async-done(((bf16[3,8,48,4096]{3,2,1,0:T(8,128)(2,1)}), bf16[3,8,384,4096]{3,2,1,0:T(8,128)(2,1)}) %all-gather.2.cloned.1.call-update) | async-done | bytes 75497488 | tf_op jit(solution)/shard_map/all_gather | solution.py:156
  784.7 74.7 %copy.91 = f32[1152,8,32,128]{3,2,1,0:T(8,128)} copy(bf16[1152,8,32,128]{3,1,2,0:T(8,128)(2,1)} %bitcast.100) | data formatting | bytes 226492416
  859.4 73.6 %multiply_convert_fusion = bf16[3,8,384,32,128]{4,3,2,1,0:T(8,128)(2,1)} fusion(f32[3,8,384,32,128]{4,3,2,1,0:T(8,128)} %bitcast.53, f32[3,8,384,32]{3,2,1,0:T(8,128)} %copy.71), kind=kLoop, calls=%fused_computation | loop fusion | flops 75497472 | bytes 227672064 | tf_op jit(solution)/shard_map/convert_element_type | solution.py:46
  933.1 50.2 %fusion.122 = (bf16[1,8,384,32,128]{4,3,2,1,0:T(8,128)(2,1)}, bf16[1,8,384,32,128]{4,3,2,1,0:T(8,128)(2,1)}, bf16[1,8,384,32,128]{4,3,2,1,0:T(8,128)(2,1)}) fusion(bf16[3,8,384,32,128]{4,3,2,1,0:T(8,128)(2,1)} %multiply_convert_fusion), kind=kLoop, calls=%fused_computation.179 | loop fusion | bytes 150994944 | tf_op jit(solution)/shard_map/slice | solution.py:113
  983.3 37.3 %squeeze.16 = bf16[8,384,4096]{2,1,0:T(8,128)(2,1)} reshape(bf16[1,8,384,32,128]{4,3,2,1,0:T(8,128)(2,1)} %get-tuple-element.19) | data formatting | bytes 50331648 | tf_op jit(solution)/shard_map/squeeze | solution.py:113
  1020.6 37.4 %squeeze.7 = bf16[8,384,4096]{2,1,0:T(8,128)(2,1)} reshape(bf16[1,8,384,32,128]{4,3,2,1,0:T(8,128)(2,1)} %get-tuple-element.20) | data formatting | bytes 50331648 | tf_op jit(solution)/shard_map/squeeze | solution.py:113
  1058.0 37.3 %squeeze.6 = bf16[8,384,4096]{2,1,0:T(8,128)(2,1)} reshape(bf16[1,8,384,32,128]{4,3,2,1,0:T(8,128)(2,1)} %get-tuple-element.18) | data formatting | bytes 50331648 | tf_op jit(solution)/shard_map/squeeze | solution.py:113
  1095.3 11.5 fusion.126
  1106.9 18.2 %fusion.34 = f32[8,8,4096]{2,1,0:T(8,128)S(1)} fusion(bf16[8,384,4096]{2,1,0:T(8,128)(2,1)} %squeeze.16, bf16[8,8,4096]{2,1,0:T(8,128)(2,1)S(1)} %copy-done, bf16[8,384,4096]{2,1,0:T(8,128)(2,1)} %squeeze.7, f32[8,8,384]{2,1,0:T(8,128)S(1)} %fusion.126), kind=kOutput, calls=%fused_computation.35 | convolution fusion | flops 402800640 | bytes 52002816 | tf_op jit(solution)/shard_map/ech,ehd->ecd/dot_general | solution.py:109
  1125.1 2.6 convolution_bitcast_fusion.1
  1127.9 0.2 reduce_window_sum.18
  1128.2 26.0 %reduce-scatter.7.cloned.1.call-done = f32[64,1024]{1,0:T(8,128)} async-done(((f32[64,4096]{1,0:T(8,128)}), f32[64,1024]{1,0:T(8,128)}) %reduce-scatter.7.cloned.1.call-update) | async-done | bytes 262160 | tf_op jit(solution)/shard_map/reduce_scatter | solution.py:189
  1154.1 1.2 fusion.53
  1155.3 8.9 psum.15
  1164.4 10.2 all_gather.11
  1174.6 0.3 convolution_convert_fusion
  1174.9 11.5 fusion.128
  1186.4 18.2 %fusion.32 = f32[8,8,4096]{2,1,0:T(8,128)S(1)} fusion(bf16[8,384,4096]{2,1,0:T(8,128)(2,1)} %squeeze.16, bf16[8,8,4096]{2,1,0:T(8,128)(2,1)S(1)} %convolution_convert_fusion, bf16[8,384,4096]{2,1,0:T(8,128)(2,1)} %squeeze.7, f32[8,8,384]{2,1,0:T(8,128)S(1)} %fusion.128), kind=kOutput, calls=%fused_computation.32 | convolution fusion | flops 402800640 | bytes 52002816 | tf_op jit(solution)/shard_map/ech,ehd->ecd/dot_general | solution.py:109
  1204.6 2.6 convolution_bitcast_fusion
  1207.2 0.7 copy.80
  1208.0 27.3 %reduce-scatter.11.cloned.1.call-done = f32[64,1024]{1,0:T(8,128)} async-done(((f32[64,4096]{1,0:T(8,128)}), f32[64,1024]{1,0:T(8,128)}) %reduce-scatter.11.cloned.1.call-update) | async-done | bytes 262160 | tf_op jit(solution)/shard_map/reduce_scatter | solution.py:189
  1235.3 1.6 fusion.56
  (94 shorter events, 1.5 us)
Async XLA Ops:
  9.1 5.3 copy-start.6
  14.4 1.0 copy-start.5
  18.9 20.3 %slice-start = ((s8[6291456]{0:T(1024)(128)(4,1)}), s8[2097152]{0:T(1024)(128)(4,1)S(1)}, s32[]{:S(2)}) async-start(s8[6291456]{0:T(1024)(128)(4,1)} %bitcast.150), calls=%async_computation.11 | async-start | bytes 4194304
  25.8 93.9 %all-to-all-start = ((bf16[16,4,2048]{2,0,1:T(8,128)(2,1)}), bf16[16,4,2048]{2,0,1:T(8,128)(2,1)S(1)}, u32[]{:S(2)}, u32[]{:S(2)}) async-start(bf16[16,4,2048]{2,0,1:T(8,128)(2,1)} %copy.67), calls=%async_computation | async-start | bytes 524288 | tf_op jit(solution)/shard_map/all_to_all | solution.py:170
  31.0 151.2 %reduce-scatter.5.cloned.1.call-start = ((), (), s32[]{:S(2)}) async-start(), calls=%async_computation.6 | async-start | bytes 1310720 | tf_op jit(solution)/shard_map/reduce_scatter | solution.py:174
  31.0 8.3 slice-start.1
  91.3 69.1 %copy-start.1 = (f32[3,8,12,32]{3,2,1,0:T(8,128)}, f32[3,8,12,32]{3,2,1,0:T(8,128)S(1)}, u32[]{:S(2)}) copy-start(f32[3,8,12,32]{3,2,1,0:T(8,128)S(1)} %pmax.7) | copy-start | bytes 110596
  129.5 655.3 %all-gather.2.cloned.1.call-start = ((), (), s32[]{:S(2)}) async-start(), calls=%async_computation.7 | async-start | bytes 84934656 | tf_op jit(solution)/shard_map/all_gather | solution.py:156
  129.5 22.3 %copy-start.9 = (bf16[2,16,512]{2,1,0:T(8,128)(2,1)S(1)}, bf16[2,16,512]{2,1,0:T(8,128)(2,1)}, u32[]{:S(2)}) copy-start(bf16[2,16,512]{2,1,0:T(8,128)(2,1)} %param.18) | copy-start | bytes 98308
  129.5 22.3 %copy-start.8 = (bf16[2,16,512]{2,1,0:T(8,128)(2,1)S(1)}, bf16[2,16,512]{2,1,0:T(8,128)(2,1)}, u32[]{:S(2)}) copy-start(bf16[2,16,512]{2,1,0:T(8,128)(2,1)} %param.19) | copy-start | bytes 98308
  129.5 22.3 %copy-start.7 = (bf16[2,8,64,128]{3,2,1,0:T(8,128)(2,1)S(1)}, bf16[2,8,64,128]{3,2,1,0:T(8,128)(2,1)}, u32[]{:S(2)}) copy-start(bf16[2,8,64,128]{3,2,1,0:T(8,128)(2,1)} %copy-done.6) | copy-start | bytes 786436
  151.7 13.3 %copy-start.19 = (s32[2,64,8]{1,2,0:T(8,128)S(1)}, s32[2,64,8]{1,2,0:T(8,128)}, u32[]{:S(2)}) copy-start(s32[2,64,8]{1,2,0:T(8,128)} %param.21) | copy-start | bytes 12292
  151.7 14.9 %copy-start.20 = (f32[2,64,8]{1,2,0:T(8,128)S(1)}, f32[2,64,8]{1,2,0:T(8,128)}, u32[]{:S(2)}) copy-start(f32[2,64,8]{1,2,0:T(8,128)} %param.22) | copy-start | bytes 12292
  156.9 11.5 all-to-all-start.1
  160.4 967.8 %reduce-scatter.9.cloned.1.call-start = ((), (), s32[]{:S(2)}) async-start(), calls=%async_computation.9 | async-start | bytes 1310720 | tf_op jit(solution)/shard_map/reduce_scatter | solution.py:174
  165.7 16.5 %copy-start.16 = (pred[8,64]{1,0:T(8,128)(4,1)}, pred[8,64]{1,0:T(8,128)(4,1)S(1)}, u32[]{:S(2)}) copy-start(pred[8,64]{1,0:T(8,128)(4,1)S(1)} %fusion.82) | copy-start | bytes 1540
  166.6 692.8 %copy-start.10 = (f32[1024]{0:T(1024)}, f32[1024]{0:T(1024)S(1)}, u32[]{:S(2)}) copy-start(f32[1024]{0:T(1024)S(1)} %dynamic_slice.8) | copy-start | bytes 12292
  167.8 691.6 %copy-start.12 = (s32[8,64]{1,0:T(8,128)}, s32[8,64]{1,0:T(8,128)S(1)}, u32[]{:S(2)}) copy-start(s32[8,64]{1,0:T(8,128)S(1)} %broadcast_add_fusion.1) | copy-start | bytes 6148
  182.1 972.0 %reduce-scatter.7.cloned.1.call-start = ((), (), s32[]{:S(2)}) async-start(), calls=%async_computation.8 | async-start | bytes 1310720 | tf_op jit(solution)/shard_map/reduce_scatter | solution.py:189
  183.4 676.0 %copy-start.3 = (bf16[64,1024]{1,0:T(8,128)(2,1)}, bf16[64,1024]{1,0:T(8,128)(2,1)S(1)}, u32[]{:S(2)}) copy-start(bf16[64,1024]{1,0:T(8,128)(2,1)S(1)} %get-tuple-element.17) | copy-start | bytes 393220
  1058.0 37.3 %copy-start = (bf16[8,8,4096]{2,1,0:T(8,128)(2,1)S(1)}, bf16[8,8,4096]{2,1,0:T(8,128)(2,1)}, u32[]{:S(2)}) copy-start(bf16[8,8,4096]{2,1,0:T(8,128)(2,1)} %convolution_convert_fusion.1) | copy-start | bytes 1572868
  1106.8 18.3 %copy-start.13 = (s32[8,64]{1,0:T(8,128)S(1)}, s32[8,64]{1,0:T(8,128)}, u32[]{:S(2)}) copy-start(s32[8,64]{1,0:T(8,128)} %copy-done.12) | copy-start | bytes 6148
  1106.8 18.3 %copy-start.15 = (f32[8,64]{1,0:T(8,128)S(1)}, f32[8,64]{1,0:T(8,128)}, u32[]{:S(2)}) copy-start(f32[8,64]{1,0:T(8,128)} %broadcast_divide_fusion.1) | copy-start | bytes 6148
  1106.8 18.3 %copy-start.17 = (pred[8,64]{1,0:T(8,128)(4,1)S(1)}, pred[8,64]{1,0:T(8,128)(4,1)}, u32[]{:S(2)}) copy-start(pred[8,64]{1,0:T(8,128)(4,1)} %copy-done.16) | copy-start | bytes 1540
  1106.9 20.9 %copy-start.14 = (s32[64,8]{0,1:T(8,128)S(1)}, s32[64,8]{0,1:T(8,128)}, u32[]{:S(2)}) copy-start(s32[64,8]{0,1:T(8,128)} %get-tuple-element.26) | copy-start | bytes 6148
  1106.9 21.2 %copy-start.18 = (f32[64,8]{0,1:T(8,128)S(1)}, f32[64,8]{0,1:T(8,128)}, u32[]{:S(2)}) copy-start(f32[64,8]{0,1:T(8,128)} %get-tuple-element.25) | copy-start | bytes 6148
  1106.9 21.2 %copy-start.21 = (f32[64]{0:T(128)S(1)}, f32[64]{0:T(128)}, u32[]{:S(2)}) copy-start(f32[64]{0:T(128)} %get-tuple-element.10) | copy-start | bytes 772
  1106.9 47.2 %copy-start.4 = (bf16[64,1024]{1,0:T(8,128)(2,1)S(1)}, bf16[64,1024]{1,0:T(8,128)(2,1)}, u32[]{:S(2)}) copy-start(bf16[64,1024]{1,0:T(8,128)(2,1)} %copy-done.3) | copy-start | bytes 393220
  1106.9 57.3 %copy-start.11 = (f32[1024]{0:T(1024)S(1)}, f32[1024]{0:T(1024)}, u32[]{:S(2)}) copy-start(f32[1024]{0:T(1024)} %copy-done.10) | copy-start | bytes 12292
  1127.8 107.5 %reduce-scatter.11.cloned.1.call-start = ((), (), s32[]{:S(2)}) async-start(), calls=%async_computation.10 | async-start | bytes 1310720 | tf_op jit(solution)/shard_map/reduce_scatter | solution.py:189
  1186.4 20.8 %copy-start.2 = (f32[3,8,12,32]{3,2,1,0:T(8,128)S(1)}, f32[3,8,12,32]{3,2,1,0:T(8,128)}, u32[]{:S(2)}) copy-start(f32[3,8,12,32]{3,2,1,0:T(8,128)} %copy-done.1) | copy-start | bytes 110596
Sparse Core Ops, SparseCore 0:
  129.6 26.9 reduce-scatter.4
  182.2 29.3 reduce-scatter.8
  1127.9 26.2 reduce-scatter.6
  1207.3 27.9 reduce-scatter.10
Sparse Core Ops, SparseCore 1:
  151.9 632.8 all-gather.1
where the time goes:
time: 1260 us; the launch traced here: 1240 us
  waiting for transfers between devices  633 us (50%)
  local copies, waits for them, and re-layouts  286 us (23%)
  other arithmetic  111 us (9%)
  matrix products  105 us (8%)
  blocking collectives  83.5 us (7%)
  between operations  16 us (1%)
    all_gather x1, waiting for transfers between devices, local(): gathered = lax.all_gather(quantized, 'fsdp', axis=2, tiled=True)  580 us
    squeeze x3, local copies, waits for them, and re-layouts, local_experts(): outputs = expert_rows(selected, restored[0], restored[1], restored[2])  112 us
    unnamed x56, local copies, waits for them, and re-layouts  87.2 us
    convert_element_type x1, other arithmetic, dequantize(): (tiles * factors[..., None]).astype(jnp.bfloat16).reshape(3, WIN, count, D)  73.6 us
    reduce_scatter x2, waiting for transfers between devices, local(): lax.psum_scatter(partial_value, 'tp', scatter_dimension=1, tiled=True)  53.3 us
    slice x1, local copies, waits for them, and re-layouts, local_experts(): outputs = expert_rows(selected, restored[0], restored[1], restored[2])  50.2 us
    pmax x1, blocking collectives, local(): block_max = lax.pmax(partial_max, ('fsdp', 'tp'))  44 us
    dot_general x2, matrix products, expert_rows(): jnp.einsum('ech,ehd->ecd', product, down_rows, preferred_element_type=jnp...  36.4 us
  transfers between devices with their start and end apart: 7, of which 3 were waited for; matrix products, arithmetic and copies ran while one was open for 35% of the time, Pallas kernels for 0%

commit v1 on v0

--- a/solution.py
+++ b/solution.py
@@ -153,7 +153,14 @@
         .astype(jnp.bfloat16)
         .reshape(3, WIN, shard_rows, D)
     )
-    gathered = lax.all_gather(quantized, "fsdp", axis=2, tiled=True)
+    size = lax.axis_size("fsdp")
+    right = [(i, (i + 1) % size) for i in range(size)]
+    pieces = [quantized]
+    for far in range(1, size):
+        pieces = [lax.ppermute(pieces[0], "fsdp", right), *pieces]
+    result = jnp.concatenate(pieces, axis=2)
+    places_2 = (lax.axis_index("fsdp") + 1) * pieces[-1].shape[2]
+    gathered = jnp.roll(result, places_2, axis=2)
     restored = dequantize(gathered, shard_rows, tp_count, tp_pos, scales)
     share_cols = D // tp_count
     own_start = tp_pos * share_cols

time: 1260 us -> 1610 us (1.28)
  local copies, waits for them, and re-layouts: 286 us -> 445 us
  other arithmetic: 111 us -> 229 us
  waiting for transfers between devices: 633 us -> 719 us
    ppermute x0 -> x7, waiting for transfers between devices: none -> 651 us  [local(): pieces = [lax.ppermute(pieces[0], 'fsdp', right), *pieces]]
    all_gather x1 -> x0, waiting for transfers between devices: 580 us -> none  [local(): gathered = lax.all_gather(quantized, 'fsdp', axis=2, tiled=True)]
    unnamed x56 -> x78, local copies, waits for them, and re-layouts: 87.2 us -> 249 us
    reshape x0 -> x1, other arithmetic: none -> 77.8 us  [dequantize(): shard_piece.astype(jnp.float32).reshape(3, WIN, count, D // BLOCK, BLOCK)]
    unnamed x1 -> x2, other arithmetic: 0.01 us -> 22.1 us
    concatenate x0 -> x1, other arithmetic: none -> 21.9 us  [local(): gathered = jnp.roll(result, places_2, axis=2)]
  transfers between devices with their start and end apart: 7 -> 13, of which waited for: 3 -> 10; matrix products, arithmetic and copies ran while one was open for 35% -> 41% of each run, Pallas kernels for 0% -> 0%
where the time goes in v1:
time: 1610 us; the launch traced here: 1600 us
  waiting for transfers between devices  719 us (45%)
  local copies, waits for them, and re-layouts  445 us (28%)
  other arithmetic  229 us (14%)
  matrix products  101 us (6%)
  blocking collectives  84.4 us (5%)
    ppermute x7, waiting for transfers between devices, local(): pieces = [lax.ppermute(pieces[0], 'fsdp', right), *pieces]  651 us
    unnamed x78, local copies, waits for them, and re-layouts  249 us
    squeeze x3, local copies, waits for them, and re-layouts, local_experts(): outputs = expert_rows(selected, restored[0], restored[1], restored[2])  112 us
    reshape x1, other arithmetic, dequantize(): shard_piece.astype(jnp.float32).reshape(3, WIN, count, D // BLOCK, BLOCK)  77.8 us
    convert_element_type x1, other arithmetic, dequantize(): (tiles * factors[..., None]).astype(jnp.bfloat16).reshape(3, WIN, count, D)  73.6 us
    reduce_scatter x2, waiting for transfers between devices, local(): lax.psum_scatter(partial_value, 'tp', scatter_dimension=1, tiled=True)  52.2 us
    slice x1, local copies, waits for them, and re-layouts, local_experts(): outputs = expert_rows(selected, restored[0], restored[1], restored[2])  50.3 us
    pmax x1, blocking collectives, local(): block_max = lax.pmax(partial_max, ('fsdp', 'tp'))  44.7 us
  transfers between devices with their start and end apart: 13, of which 10 were waited for; matrix products, arithmetic and copies ran while one was open for 41% of the time, Pallas kernels for 0%

profile of v1, /device:TPU:0, one launch (start us, length us, event | category | flops | bytes accessed | tf_op | source)
XLA Modules:
  0.0 1601.3 jit_solution(5705239455727097145)
XLA Ops:
  7.2 4.2 copy.88
  11.5 4.1 copy.89
  16.9 5.2 fusion
  23.6 44.7 %pmax.7 = f32[3,8,12,32]{3,2,1,0:T(8,128)S(1)} all-reduce(f32[3,8,12,32]{3,2,1,0:T(8,128)S(1)} %select_reduce_fusion), channel_id=1, replica_groups=mesh['fsdp'=8,'tp'=4] {'fsdp','tp'}, use_global_device_ids=true, to_apply=%region_11.12 | all-reduce | flops 9216 | bytes 73728 | tf_op jit(solution)/shard_map/pmax | solution.py:146
  69.1 7.1 div.130
  76.2 20.4 %div.131 = f32[3,8,48,4096]{3,2,1,0:T(8,128)} reshape(f32[3,8,48,32,128]{4,3,2,1,0:T(8,128)} %div.130) | data formatting | bytes 37748736 | tf_op jit(solution)/shard_map/div | solution.py:152
  96.6 19.6 %multiply_convert_fusion.1 = bf16[3,8,48,4096]{3,2,1,0:T(8,128)(2,1)S(1)} fusion(f32[3,8,48,4096]{3,2,1,0:T(8,128)} %div.131, f32[1,8,48,4096]{3,2,1,0:T(8,128)} %bitcast.141, f32[1,8,48,4096]{3,2,1,0:T(8,128)} %bitcast.148, f32[1,8,48,4096]{3,2,1,0:T(8,128)} %bitcast.152), kind=kLoop, calls=%fused_computation.5 | loop fusion | flops 80216064 | bytes 47185920 | tf_op jit(solution)/shard_map/convert_element_type | solution.py:153
  116.3 105.9 %collective-permute-done = bf16[3,8,48,4096]{3,2,1,0:T(8,128)(2,1)S(1)} collective-permute-done((bf16[3,8,48,4096]{3,2,1,0:T(8,128)(2,1)S(1)}, bf16[3,8,48,4096]{3,2,1,0:T(8,128)(2,1)S(1)}, u32[]{:S(2)}, u32[]{:S(2)}) %collective-permute-start) | collective-permute-done | bytes 9437216 | tf_op jit(solution)/shard_map/ppermute | solution.py:160
  222.2 3.6 copy-done
  225.9 105.9 %collective-permute-done.1 = bf16[3,8,48,4096]{3,2,1,0:T(8,128)(2,1)S(1)} collective-permute-done((bf16[3,8,48,4096]{3,2,1,0:T(8,128)(2,1)S(1)}, bf16[3,8,48,4096]{3,2,1,0:T(8,128)(2,1)S(1)}, u32[]{:S(2)}, u32[]{:S(2)}) %collective-permute-start.1) | collective-permute-done | bytes 9437216 | tf_op jit(solution)/shard_map/ppermute | solution.py:160
  331.8 3.6 copy-done.1
  335.4 105.9 %collective-permute-done.2 = bf16[3,8,48,4096]{3,2,1,0:T(8,128)(2,1)S(1)} collective-permute-done((bf16[3,8,48,4096]{3,2,1,0:T(8,128)(2,1)S(1)}, bf16[3,8,48,4096]{3,2,1,0:T(8,128)(2,1)S(1)}, u32[]{:S(2)}, u32[]{:S(2)}) %collective-permute-start.2) | collective-permute-done | bytes 9437216 | tf_op jit(solution)/shard_map/ppermute | solution.py:160
  441.3 3.6 copy-done.2
  444.9 105.9 %collective-permute-done.3 = bf16[3,8,48,4096]{3,2,1,0:T(8,128)(2,1)S(1)} collective-permute-done((bf16[3,8,48,4096]{3,2,1,0:T(8,128)(2,1)S(1)}, bf16[3,8,48,4096]{3,2,1,0:T(8,128)(2,1)S(1)}, u32[]{:S(2)}, u32[]{:S(2)}) %collective-permute-start.3) | collective-permute-done | bytes 9437216 | tf_op jit(solution)/shard_map/ppermute | solution.py:160
  550.8 3.6 copy-done.3
  554.4 105.9 %collective-permute-done.4 = bf16[3,8,48,4096]{3,2,1,0:T(8,128)(2,1)S(1)} collective-permute-done((bf16[3,8,48,4096]{3,2,1,0:T(8,128)(2,1)S(1)}, bf16[3,8,48,4096]{3,2,1,0:T(8,128)(2,1)S(1)}, u32[]{:S(2)}, u32[]{:S(2)}) %collective-permute-start.4) | collective-permute-done | bytes 9437216 | tf_op jit(solution)/shard_map/ppermute | solution.py:160
  660.3 3.7 copy-done.4
  664.0 106.0 %collective-permute-done.5 = bf16[3,8,48,4096]{3,2,1,0:T(8,128)(2,1)} collective-permute-done((bf16[3,8,48,4096]{3,2,1,0:T(8,128)(2,1)S(1)}, bf16[3,8,48,4096]{3,2,1,0:T(8,128)(2,1)}, u32[]{:S(2)}, u32[]{:S(2)}) %collective-permute-start.5) | collective-permute-done | bytes 9437216 | tf_op jit(solution)/shard_map/ppermute | solution.py:160
  770.6 3.5 select_reduce_fusion.2
  774.1 3.5 fusion.37
  777.7 3.0 fusion.28
  781.6 3.8 all-to-all-start
  786.7 3.0 fusion.25
  790.4 3.0 copy.71
  794.3 4.2 all-to-all-start.1
  798.4 9.7 fusion.125
  812.2 10.0 fusion.127
  822.2 15.0 reduce-scatter.5.cloned.1.call-done
  838.3 8.9 psum.14
  847.3 11.9 all_gather.6
  860.3 16.0 collective-permute-done.6
  876.3 8.6 constant_dynamic-update-slice_fusion.15
  884.9 8.6 constant_dynamic-update-slice_fusion.14
  893.4 8.7 constant_dynamic-update-slice_fusion.13
  902.1 8.6 constant_dynamic-update-slice_fusion.12
  910.7 8.6 constant_dynamic-update-slice_fusion.11
  919.3 8.6 constant_dynamic-update-slice_fusion.10
  927.9 8.6 constant_dynamic-update-slice_fusion.9
  936.5 22.1 %constant_dynamic-update-slice_fusion.8 = bf16[3,8,768,4096]{3,2,1,0:T(8,128)(2,1)} fusion(bf16[3,8,768,4096]{3,2,1,0:T(8,128)(2,1)} %constant_dynamic-update-slice_fusion.9, f32[3,8,48,4096]{3,2,1,0:T(8,128)} %div.131, f32[1,8,48,4096]{3,2,1,0:T(8,128)} %bitcast.142, f32[1,8,48,4096]{3,2,1,0:T(8,128)} %bitcast.149, f32[1,8,48,4096]{3,2,1,0:T(8,128)} %bitcast.153), kind=kLoop, calls=%fused_computation.104 | loop fusion | flops 80216064 | bytes 47185920
  958.6 8.7 constant_dynamic-update-slice_fusion.7
  967.3 8.7 constant_dynamic-update-slice_fusion.6
  976.0 8.7 constant_dynamic-update-slice_fusion.5
  984.6 8.6 constant_dynamic-update-slice_fusion.4
  993.3 8.8 constant_dynamic-update-slice_fusion.3
  1002.0 8.7 constant_dynamic-update-slice_fusion.2
  1010.7 8.6 constant_dynamic-update-slice_fusion.1
  1019.3 21.9 %constant_dynamic-update-slice_fusion = bf16[3,8,768,4096]{3,2,1,0:T(8,128)(2,1)} fusion(bf16[3,8,768,4096]{3,2,1,0:T(8,128)(2,1)} %constant_dynamic-update-slice_fusion.1, f32[3,8,48,4096]{3,2,1,0:T(8,128)} %div.131, f32[1,8,48,4096]{3,2,1,0:T(8,128)} %bitcast.143, f32[1,8,48,4096]{3,2,1,0:T(8,128)} %bitcast.150, f32[1,8,48,4096]{3,2,1,0:T(8,128)} %bitcast.154), kind=kLoop, calls=%fused_computation.96 | loop fusion | flops 80216064 | bytes 47185920 | tf_op jit(solution)/shard_map/jit(_roll_dynamic)/concatenate | solution.py:163
  1041.2 77.8 %dynamic-slice_convert_fusion = f32[3,8,384,4096]{3,2,1,0:T(8,128)} fusion(bf16[3,8,768,4096]{3,2,1,0:T(8,128)(2,1)} %constant_dynamic-update-slice_fusion, s32[]{:T(128)S(6)} %select_n.84), kind=kLoop, calls=%fused_computation.1 | loop fusion | flops 37748736 | bytes 226492416 | tf_op jit(solution)/shard_map/reshape | solution.py:45
  1119.0 98.8 %copy.91 = f32[1152,8,32,128]{3,2,1,0:T(8,128)} copy(f32[1152,8,32,128]{3,1,2,0:T(8,128)} %bitcast.51) | data formatting | bytes 301989888
  1217.8 73.6 %multiply_convert_fusion = bf16[3,8,384,32,128]{4,3,2,1,0:T(8,128)(2,1)} fusion(f32[3,8,384,32,128]{4,3,2,1,0:T(8,128)} %bitcast.53, f32[3,8,384,32]{3,2,1,0:T(8,128)} %copy.71), kind=kLoop, calls=%fused_computation | loop fusion | flops 75497472 | bytes 227672064 | tf_op jit(solution)/shard_map/convert_element_type | solution.py:46
  1291.5 50.3 %fusion.122 = (bf16[1,8,384,32,128]{4,3,2,1,0:T(8,128)(2,1)}, bf16[1,8,384,32,128]{4,3,2,1,0:T(8,128)(2,1)}, bf16[1,8,384,32,128]{4,3,2,1,0:T(8,128)(2,1)}) fusion(bf16[3,8,384,32,128]{4,3,2,1,0:T(8,128)(2,1)} %multiply_convert_fusion), kind=kLoop, calls=%fused_computation.196 | loop fusion | bytes 150994944 | tf_op jit(solution)/shard_map/slice | solution.py:113
  1341.7 37.3 %squeeze.6 = bf16[8,384,4096]{2,1,0:T(8,128)(2,1)} reshape(bf16[1,8,384,32,128]{4,3,2,1,0:T(8,128)(2,1)} %get-tuple-element.18) | data formatting | bytes 50331648 | tf_op jit(solution)/shard_map/squeeze | solution.py:113
  1379.1 37.4 %squeeze.16 = bf16[8,384,4096]{2,1,0:T(8,128)(2,1)} reshape(bf16[1,8,384,32,128]{4,3,2,1,0:T(8,128)(2,1)} %get-tuple-element.19) | data formatting | bytes 50331648 | tf_op jit(solution)/shard_map/squeeze | solution.py:113
  1416.4 37.3 %squeeze.7 = bf16[8,384,4096]{2,1,0:T(8,128)(2,1)} reshape(bf16[1,8,384,32,128]{4,3,2,1,0:T(8,128)(2,1)} %get-tuple-element.20) | data formatting | bytes 50331648 | tf_op jit(solution)/shard_map/squeeze | solution.py:113
  1453.8 11.5 fusion.126
  1465.3 18.2 %fusion.34 = f32[8,8,4096]{2,1,0:T(8,128)S(1)} fusion(bf16[8,384,4096]{2,1,0:T(8,128)(2,1)} %squeeze.16, bf16[8,8,4096]{2,1,0:T(8,128)(2,1)S(1)} %copy-done.5, bf16[8,384,4096]{2,1,0:T(8,128)(2,1)} %squeeze.7, f32[8,8,384]{2,1,0:T(8,128)S(1)} %fusion.126), kind=kOutput, calls=%fused_computation.36 | convolution fusion | flops 402800640 | bytes 52002816 | tf_op jit(solution)/shard_map/ech,ehd->ecd/dot_general | solution.py:109
  1483.5 2.6 convolution_bitcast_fusion.1
  1486.6 24.9 %reduce-scatter.7.cloned.1.call-done = f32[64,1024]{1,0:T(8,128)} async-done(((f32[64,4096]{1,0:T(8,128)}), f32[64,1024]{1,0:T(8,128)}) %reduce-scatter.7.cloned.1.call-update) | async-done | bytes 262160 | tf_op jit(solution)/shard_map/reduce_scatter | solution.py:196
  1512.7 8.9 psum.15
  1521.8 10.0 all_gather.7
  1532.1 11.8 fusion.128
  1543.8 18.2 %fusion.32 = f32[8,8,4096]{2,1,0:T(8,128)S(1)} fusion(bf16[8,384,4096]{2,1,0:T(8,128)(2,1)} %squeeze.16, bf16[8,8,4096]{2,1,0:T(8,128)(2,1)S(1)} %convolution_convert_fusion, bf16[8,384,4096]{2,1,0:T(8,128)(2,1)} %squeeze.7, f32[8,8,384]{2,1,0:T(8,128)S(1)} %fusion.128), kind=kOutput, calls=%fused_computation.33 | convolution fusion | flops 402800640 | bytes 52002816 | tf_op jit(solution)/shard_map/ech,ehd->ecd/dot_general | solution.py:109
  1562.0 2.6 convolution_bitcast_fusion
  1565.4 27.3 %reduce-scatter.11.cloned.1.call-done = f32[64,1024]{1,0:T(8,128)} async-done(((f32[64,4096]{1,0:T(8,128)}), f32[64,1024]{1,0:T(8,128)}) %reduce-scatter.11.cloned.1.call-update) | async-done | bytes 262160 | tf_op jit(solution)/shard_map/reduce_scatter | solution.py:196
  (131 shorter events, 18.7 us)
Async XLA Ops:
  7.2 8.4 slice-start
  7.2 8.3 slice-start.1
  68.3 721.3 %copy-start.6 = (f32[3,8,12,32]{3,2,1,0:T(8,128)}, f32[3,8,12,32]{3,2,1,0:T(8,128)S(1)}, u32[]{:S(2)}) copy-start(f32[3,8,12,32]{3,2,1,0:T(8,128)S(1)} %pmax.7) | copy-start | bytes 110596
  96.6 673.5 %copy-start.10 = (bf16[2,16,8192]{2,1,0:T(8,128)(2,1)S(1)}, bf16[2,16,8192]{2,1,0:T(8,128)(2,1)}, u32[]{:S(2)}) copy-start(bf16[2,16,8192]{2,1,0:T(8,128)(2,1)} %param.15) | copy-start | bytes 1572868
  96.6 673.5 %slice-start.2 = ((bf16[2,16,512]{2,1,0:T(8,128)(2,1)}), bf16[1,16,512]{2,1,0:T(8,128)(2,1)S(1)}, s32[]{:S(2)}) async-start(bf16[2,16,512]{2,1,0:T(8,128)(2,1)} %param.18), calls=%async_computation.12 | async-start | bytes 32768 | tf_op jit(solution)/shard_map/slice | solution.py:173
  96.6 673.6 %copy-start.11 = (bf16[2,16,512]{2,1,0:T(8,128)(2,1)S(1)}, bf16[2,16,512]{2,1,0:T(8,128)(2,1)}, u32[]{:S(2)}) copy-start(bf16[2,16,512]{2,1,0:T(8,128)(2,1)} %param.19) | copy-start | bytes 98308
  96.6 673.7 %copy-start.25 = (s32[16]{0:T(128)S(1)}, s32[16]{0:T(128)}, u32[]{:S(2)}) copy-start(s32[16]{0:T(128)} %param.20) | copy-start | bytes 196
  116.3 669.2 %copy-start.12 = (bf16[2,16,512]{2,1,0:T(8,128)(2,1)S(1)}, bf16[2,16,512]{2,1,0:T(8,128)(2,1)}, u32[]{:S(2)}) copy-start(bf16[2,16,512]{2,1,0:T(8,128)(2,1)} %param.18) | copy-start | bytes 98308
  116.3 106.0 %collective-permute-start = (bf16[3,8,48,4096]{3,2,1,0:T(8,128)(2,1)S(1)}, bf16[3,8,48,4096]{3,2,1,0:T(8,128)(2,1)S(1)}, u32[]{:S(2)}, u32[]{:S(2)}) collective-permute-start(bf16[3,8,48,4096]{3,2,1,0:T(8,128)(2,1)S(1)} %multiply_convert_fusion.1), channel_id=1, source_target_pairs={{0,4},{4,8},{8,12},{12,16},{16,20},{20,24},{24,28},{28,0},{1,5},{5... | collective-permute-start | bytes 28311560 | tf_op jit(solution)/shard_map/ppermute | solution.py:160
  222.2 3.6 copy-start
  225.9 105.9 %collective-permute-start.1 = (bf16[3,8,48,4096]{3,2,1,0:T(8,128)(2,1)S(1)}, bf16[3,8,48,4096]{3,2,1,0:T(8,128)(2,1)S(1)}, u32[]{:S(2)}, u32[]{:S(2)}) collective-permute-start(bf16[3,8,48,4096]{3,2,1,0:T(8,128)(2,1)S(1)} %collective-permute-done), channel_id=1, source_target_pairs={{0,4},{4,8},{8,12},{12,16},{16,20},{20,24},{24,28},{28,0},{1,5},{5... | collective-permute-start | bytes 28311560 | tf_op jit(solution)/shard_map/ppermute | solution.py:160
  331.8 3.6 copy-start.1
  335.4 105.9 %collective-permute-start.2 = (bf16[3,8,48,4096]{3,2,1,0:T(8,128)(2,1)S(1)}, bf16[3,8,48,4096]{3,2,1,0:T(8,128)(2,1)S(1)}, u32[]{:S(2)}, u32[]{:S(2)}) collective-permute-start(bf16[3,8,48,4096]{3,2,1,0:T(8,128)(2,1)S(1)} %collective-permute-done.1), channel_id=1, source_target_pairs={{0,4},{4,8},{8,12},{12,16},{16,20},{20,24},{24,28},{28,0},{1,5},{5... | collective-permute-start | bytes 28311560 | tf_op jit(solution)/shard_map/ppermute | solution.py:160
  441.3 3.6 copy-start.2
  444.9 105.9 %collective-permute-start.3 = (bf16[3,8,48,4096]{3,2,1,0:T(8,128)(2,1)S(1)}, bf16[3,8,48,4096]{3,2,1,0:T(8,128)(2,1)S(1)}, u32[]{:S(2)}, u32[]{:S(2)}) collective-permute-start(bf16[3,8,48,4096]{3,2,1,0:T(8,128)(2,1)S(1)} %collective-permute-done.2), channel_id=1, source_target_pairs={{0,4},{4,8},{8,12},{12,16},{16,20},{20,24},{24,28},{28,0},{1,5},{5... | collective-permute-start | bytes 28311560 | tf_op jit(solution)/shard_map/ppermute | solution.py:160
  550.8 3.6 copy-start.3
  554.4 105.9 %collective-permute-start.4 = (bf16[3,8,48,4096]{3,2,1,0:T(8,128)(2,1)S(1)}, bf16[3,8,48,4096]{3,2,1,0:T(8,128)(2,1)S(1)}, u32[]{:S(2)}, u32[]{:S(2)}) collective-permute-start(bf16[3,8,48,4096]{3,2,1,0:T(8,128)(2,1)S(1)} %collective-permute-done.3), channel_id=1, source_target_pairs={{0,4},{4,8},{8,12},{12,16},{16,20},{20,24},{24,28},{28,0},{1,5},{5... | collective-permute-start | bytes 28311560 | tf_op jit(solution)/shard_map/ppermute | solution.py:160
  660.3 3.7 copy-start.4
  664.0 106.0 %collective-permute-start.5 = (bf16[3,8,48,4096]{3,2,1,0:T(8,128)(2,1)S(1)}, bf16[3,8,48,4096]{3,2,1,0:T(8,128)(2,1)}, u32[]{:S(2)}, u32[]{:S(2)}) collective-permute-start(bf16[3,8,48,4096]{3,2,1,0:T(8,128)(2,1)S(1)} %collective-permute-done.4), channel_id=1, source_target_pairs={{0,4},{4,8},{8,12},{12,16},{16,20},{20,24},{24,28},{28,0},{1,5},{5... | collective-permute-start | bytes 28311560 | tf_op jit(solution)/shard_map/ppermute | solution.py:160
  770.0 106.2 %collective-permute-start.6 = (bf16[3,8,48,4096]{3,2,1,0:T(8,128)(2,1)}, bf16[3,8,48,4096]{3,2,1,0:T(8,128)(2,1)}, u32[]{:S(2)}, u32[]{:S(2)}) collective-permute-start(bf16[3,8,48,4096]{3,2,1,0:T(8,128)(2,1)} %collective-permute-done.5), channel_id=1, source_target_pairs={{0,4},{4,8},{8,12},{12,16},{16,20},{20,24},{24,28},{28,0},{1,5},{5... | collective-permute-start | bytes 28311560 | tf_op jit(solution)/shard_map/ppermute | solution.py:160
  781.6 12.7 all-to-all-start
  789.7 18.6 %copy-start.22 = (s32[2,64,8]{1,2,0:T(8,128)S(1)}, s32[2,64,8]{1,2,0:T(8,128)}, u32[]{:S(2)}) copy-start(s32[2,64,8]{1,2,0:T(8,128)} %param.21) | copy-start | bytes 12292
  789.7 20.1 %copy-start.23 = (f32[2,64,8]{1,2,0:T(8,128)S(1)}, f32[2,64,8]{1,2,0:T(8,128)}, u32[]{:S(2)}) copy-start(f32[2,64,8]{1,2,0:T(8,128)} %param.22) | copy-start | bytes 12292
  794.3 17.9 %all-to-all-start.1 = ((bf16[16,4,2048]{2,0,1:T(8,128)(2,1)}), bf16[16,4,2048]{2,0,1:T(8,128)(2,1)S(1)}, u32[]{:S(2)}, u32[]{:S(2)}) async-start(bf16[16,4,2048]{2,0,1:T(8,128)(2,1)} %copy.77), calls=%async_computation.3 | async-start | bytes 524288 | tf_op jit(solution)/shard_map/all_to_all | solution.py:177
  798.4 38.7 %reduce-scatter.5.cloned.1.call-start = ((), (), s32[]{:S(2)}) async-start(), calls=%async_computation.6 | async-start | bytes 1310720 | tf_op jit(solution)/shard_map/reduce_scatter | solution.py:181
  808.2 678.4 %reduce-scatter.9.cloned.1.call-start = ((), (), s32[]{:S(2)}) async-start(), calls=%async_computation.8 | async-start | bytes 1310720 | tf_op jit(solution)/shard_map/reduce_scatter | solution.py:181
  808.9 76.0 %copy-start.19 = (pred[8,64]{1,0:T(8,128)(4,1)}, pred[8,64]{1,0:T(8,128)(4,1)S(1)}, u32[]{:S(2)}) copy-start(pred[8,64]{1,0:T(8,128)(4,1)S(1)} %fusion.82) | copy-start | bytes 1540
  809.8 75.0 %copy-start.13 = (f32[1024]{0:T(1024)}, f32[1024]{0:T(1024)S(1)}, u32[]{:S(2)}) copy-start(f32[1024]{0:T(1024)S(1)} %dynamic_slice.12) | copy-start | bytes 12292
  811.0 0.6 copy-start.15
  822.1 689.4 %reduce-scatter.7.cloned.1.call-start = ((), (), s32[]{:S(2)}) async-start(), calls=%async_computation.7 | async-start | bytes 1310720 | tf_op jit(solution)/shard_map/reduce_scatter | solution.py:196
  838.3 55.1 %copy-start.8 = (bf16[64,1024]{1,0:T(8,128)(2,1)}, bf16[64,1024]{1,0:T(8,128)(2,1)S(1)}, u32[]{:S(2)}) copy-start(bf16[64,1024]{1,0:T(8,128)(2,1)S(1)} %get-tuple-element.17) | copy-start | bytes 393220
  1416.4 37.3 %copy-start.5 = (bf16[8,8,4096]{2,1,0:T(8,128)(2,1)S(1)}, bf16[8,8,4096]{2,1,0:T(8,128)(2,1)}, u32[]{:S(2)}) copy-start(bf16[8,8,4096]{2,1,0:T(8,128)(2,1)} %convolution_convert_fusion.1) | copy-start | bytes 1572868
  1465.3 18.3 %copy-start.16 = (s32[8,64]{1,0:T(8,128)S(1)}, s32[8,64]{1,0:T(8,128)}, u32[]{:S(2)}) copy-start(s32[8,64]{1,0:T(8,128)} %copy-done.15) | copy-start | bytes 6148
  1465.3 18.3 %copy-start.18 = (f32[8,64]{1,0:T(8,128)S(1)}, f32[8,64]{1,0:T(8,128)}, u32[]{:S(2)}) copy-start(f32[8,64]{1,0:T(8,128)} %broadcast_divide_fusion.1) | copy-start | bytes 6148
  1465.3 18.3 %copy-start.20 = (pred[8,64]{1,0:T(8,128)(4,1)S(1)}, pred[8,64]{1,0:T(8,128)(4,1)}, u32[]{:S(2)}) copy-start(pred[8,64]{1,0:T(8,128)(4,1)} %copy-done.19) | copy-start | bytes 1540
  1465.3 21.0 %copy-start.17 = (s32[64,8]{0,1:T(8,128)S(1)}, s32[64,8]{0,1:T(8,128)}, u32[]{:S(2)}) copy-start(s32[64,8]{0,1:T(8,128)} %get-tuple-element.26) | copy-start | bytes 6148
  1465.3 21.2 %copy-start.21 = (f32[64,8]{0,1:T(8,128)S(1)}, f32[64,8]{0,1:T(8,128)}, u32[]{:S(2)}) copy-start(f32[64,8]{0,1:T(8,128)} %get-tuple-element.25) | copy-start | bytes 6148
  1465.3 21.2 %copy-start.24 = (f32[64]{0:T(128)S(1)}, f32[64]{0:T(128)}, u32[]{:S(2)}) copy-start(f32[64]{0:T(128)} %get-tuple-element.10) | copy-start | bytes 772
  1465.3 46.2 %copy-start.9 = (bf16[64,1024]{1,0:T(8,128)(2,1)S(1)}, bf16[64,1024]{1,0:T(8,128)(2,1)}, u32[]{:S(2)}) copy-start(bf16[64,1024]{1,0:T(8,128)(2,1)} %copy-done.8) | copy-start | bytes 393220
  1465.3 56.4 %copy-start.14 = (f32[1024]{0:T(1024)S(1)}, f32[1024]{0:T(1024)}, u32[]{:S(2)}) copy-start(f32[1024]{0:T(1024)} %copy-done.13) | copy-start | bytes 12292
  1486.2 106.5 %reduce-scatter.11.cloned.1.call-start = ((), (), s32[]{:S(2)}) async-start(), calls=%async_computation.9 | async-start | bytes 1310720 | tf_op jit(solution)/shard_map/reduce_scatter | solution.py:196
  1543.8 20.8 %copy-start.7 = (f32[3,8,12,32]{3,2,1,0:T(8,128)S(1)}, f32[3,8,12,32]{3,2,1,0:T(8,128)}, u32[]{:S(2)}) copy-start(f32[3,8,12,32]{3,2,1,0:T(8,128)} %copy-done.6) | copy-start | bytes 110596
Sparse Core Ops, SparseCore 0:
  808.3 28.7 reduce-scatter.4
  840.0 29.9 reduce-scatter.8
  1486.3 25.1 reduce-scatter.6
  1564.7 27.8 reduce-scatter.10
